TPU v7x, 32 devices: a whole 2x2x4 slice. The times are simulated.
32 devices in a mesh: slab: 8 (over z, y), plane: 4 (over x, core).
Axes of the slice: x: 2, y: 2, z: 4, core: 2. Of those that a mesh axis runs over, the one named last changes fastest.
Arguments:
- a_blocks: bfloat16 [4, 96, 7, 128, 128], P('plane', 'slab'), may hold values from -0.1875 to 0.1875
- a_cols: int32 [4, 96, 7], P('plane', 'slab'), may hold values from 0 to 95, as said below
- p_blocks: bfloat16 [4, 96, 4, 128, 128], P('plane', 'slab'), may hold values from -0.75 to 0.75
- p_cols: int32 [4, 96, 4], replicated, may hold values from 0 to 31, as said below
- coarse_slot: int32 [8, 4], replicated, may hold values from 0 to 3, each once within a row
Outputs:
- coarse_op: float32 [4, 8, 128, 2560], P('plane', 'slab')
Inputs may be any that keep to these rules, and one draw needn't show every extreme that they name: `a_cols`: row g = s*12 + r of column p names 7 distinct block rows of column p, among them g itself; they lie in s*12 to s*12 + 11, or, if r < 4, in the 4 rows just below s*12, or, if r >= 8, in the 4 rows from (s+1)*12 on. `p_cols`: row g = s*12 + r names 4 distinct coarse blocks of s*4 to s*4 + 3, or, if r < 4, also of the 4 blocks before, or, if r >= 8, of the 4 blocks after. `coarse_slot`: each row is a permutation of 0 to 3.
All inputs are finite; a program needn't handle non-finite values.
Results may differ from a plain program's by a relative error of at most 0.0029.
Values may be sent and summed in bfloat16 or wider, within the bound.
A program may use at most 192 MiB of HBM per device.

v0:
```python
import jax
import jax.numpy as jnp
from jax import lax
from jax.sharding import PartitionSpec as P

GHOST = 4


def with_halo(shard, sides, width):
    for axis, dim in sides:
        count, length = (lax.axis_size(axis), shard.shape[dim])
        up = [(i, (i + 1) % count) for i in range(count - 1)]
        down = [(j, i) for i, j in up]
        last = lax.slice_in_dim(shard, length - width, length, axis=dim)
        leading = lax.slice_in_dim(shard, 0, width, axis=dim)
        before = lax.ppermute(last, axis, up)
        after = lax.ppermute(leading, axis, down)
        shard = jnp.concatenate([before, shard, after], axis=dim)
    return shard


def passed_along(shard, axis, by):
    count = lax.axis_size(axis)
    pairs = [(i, i + by) for i in range(count) if 0 <= i + by < count]
    return lax.ppermute(shard, axis, pairs)


def window_rows(blocks, cols, nearby, slab, coarse):
    count = blocks.shape[0]
    block = blocks.shape[2]
    relative = cols - (slab - 1) * coarse
    choose = (
        relative[:, :, None] == jnp.arange(3 * coarse, dtype=jnp.int32)[None, None, :]
    ).astype(jnp.int32)
    slot = jnp.sum(choose * nearby[None, None, :], axis=-1)
    place = relative // coarse * coarse + slot
    onehot = (place[:, :, None] == jnp.arange(3 * coarse, dtype=jnp.int32)[None, None, :]).astype(
        jnp.bfloat16
    )
    dense = jnp.einsum("nkw,nkab->nawb", onehot, blocks, preferred_element_type=jnp.float32)
    return dense.reshape(count, block, 3 * coarse * block).astype(jnp.bfloat16)


def on_device(a_blocks, a_cols, p_blocks, p_cols, coarse_slot):
    rows_here = a_blocks.shape[1]
    links = a_blocks.shape[2]
    block = a_blocks.shape[3]
    coarse = coarse_slot.shape[1]
    owned = coarse // lax.axis_size("plane")
    width = 3 * coarse * block
    slab = lax.axis_index("slab")
    column = lax.axis_index("plane")
    start = slab * rows_here
    ghosted = with_halo(p_blocks, (("slab", 1),), GHOST)[0]
    mine = lax.dynamic_slice_in_dim(p_cols, column, 1, 0)[0]
    mine = jnp.pad(mine, ((GHOST, GHOST), (0, 0)))
    near_cols = lax.dynamic_slice_in_dim(mine, start, rows_here + 2 * GHOST, 0)
    padded_slots = jnp.pad(coarse_slot, ((1, 1), (0, 0)))
    nearby = lax.dynamic_slice_in_dim(padded_slots, slab, 3, 0).reshape(-1)
    dense = window_rows(ghosted, near_cols, nearby, slab, coarse)
    local = a_cols[0] - (start - GHOST)
    total = jnp.zeros((rows_here, block, width), jnp.float32)
    for k in range(links):
        picked = jnp.take(dense, local[:, k], axis=0)
        total = total + jnp.einsum(
            "rab,rbw->raw", a_blocks[0, :, k], picked, preferred_element_type=jnp.float32
        )
    product = total.astype(jnp.bfloat16)
    own_rows = dense[GHOST : GHOST + rows_here].reshape(-1, width)
    partial_value = lax.dot_general(
        own_rows,
        product.reshape(-1, width),
        (((0,), (0,)), ((), ())),
        preferred_element_type=jnp.float32,
    )
    edge = coarse * block
    groups = partial_value.reshape(3, coarse * block, width)
    from_below = passed_along(groups[2], "slab", 1)
    from_above = passed_along(groups[0], "slab", -1)
    full = jnp.pad(groups[1], ((0, 0), (edge, edge)))
    full = full + jnp.pad(from_below, ((0, 0), (0, 2 * edge)))
    full = full + jnp.pad(from_above, ((0, 0), (2 * edge, 0)))
    full = full.reshape(coarse, block, 5 * coarse * block)
    result = lax.psum_scatter(full, "plane", scatter_dimension=0, tiled=True)
    return result.reshape(1, owned, block, 5 * coarse * block)


def solution(mesh):
    return jax.shard_map(
        on_device,
        mesh=mesh,
        in_specs=(
            P("plane", "slab", None, None, None),
            P("plane", "slab", None),
            P("plane", "slab", None, None, None),
            P(),
            P(),
        ),
        out_specs=P("plane", "slab", None, None),
        check_vma=False,
    )
```

profile of v0, /device:TPU:0, one launch (start us, length us, event | category | flops | bytes accessed | tf_op | source)
XLA Modules:
  0.0 384.0 jit_solution(8212572091270702240)
XLA Ops:
  6.5 0.0 copy-start
  6.5 0.0 copy-start.5
  6.5 0.0 copy-start.4
  6.5 0.0 reduce-scatter.2.cloned.1.call-start
  6.5 2.7 copy.29
  9.2 0.4 fusion.69
  9.6 4.9 %collective-permute-start = (bf16[1,4,4,128,128]{4,2,3,1,0:T(4,128)(2,1)S(1)}, bf16[1,4,4,128,128]{4,2,3,1,0:T(4,128)(2,1)S(1)}, u32[]{:S(2)}, u32[]{:S(2)}) collective-permute-start(bf16[1,4,4,128,128]{4,2,3,1,0:T(4,128)(2,1)S(1)} %get-tuple-element.23), channel_id=1, source_target_pairs={{0,4},{4,8},{8,12},{12,16},{16,20},{20,24},{24,28},{1,5},{5,9},{9,... | collective-permute-start | bytes 1572872 | tf_op jit(solution)/shard_map/ppermute | solution.py:16
  14.5 1.3 collective-permute-start.1
  15.8 0.0 copy-done.5
  15.8 0.1 pad_dynamic-slice_fusion
  15.9 0.1 copy.32
  16.0 0.1 mul.23
  16.1 0.0 copy-done.4
  16.1 0.0 copy-done
  16.2 0.1 dynamic-slice_subtract_fusion
  16.3 0.1 select_reduce_fusion
  16.3 0.1 fusion.57
  16.4 0.1 copy.33
  16.6 20.3 %collective-permute-done = bf16[1,4,4,128,128]{4,2,3,1,0:T(4,128)(2,1)S(1)} collective-permute-done((bf16[1,4,4,128,128]{4,2,3,1,0:T(4,128)(2,1)S(1)}, bf16[1,4,4,128,128]{4,2,3,1,0:T(4,128)(2,1)S(1)}, u32[]{:S(2)}, u32[]{:S(2)}) %collective-permute-start) | collective-permute-done | bytes 524320 | tf_op jit(solution)/shard_map/ppermute | solution.py:16
  36.9 0.0 collective-permute-done.1
  36.9 4.2 %convert_bitcast_fusion = bf16[20,128,12,128]{3,2,1,0:T(8,128)(2,1)S(1)} fusion(bf16[1,4,4,128,128]{4,2,3,1,0:T(4,128)(2,1)} %collective-permute-done.1, bf16[1,12,4,128,128]{4,2,3,1,0:T(4,128)(2,1)S(1)} %copy.29, bf16[1,4,4,128,128]{4,2,3,1,0:T(4,128)(2,1)S(1)} %collective-permute-done, s32[20,4]{1,0:T(8,128)S(1)} %copy.33), kind=kOutput, calls=%fused_computation.7 | convolution fusion | flops 43254720 | bytes 10486080 | tf_op jit(solution)/shard_map/nkw,nkab->nawb/dot_general | solution.py:40
  41.1 0.0 copy-start.2
  41.2 4.0 %copy-done.2 = bf16[20,128,12,128]{3,2,1,0:T(8,128)(2,1)} copy-done((bf16[20,128,12,128]{3,2,1,0:T(8,128)(2,1)}, bf16[20,128,12,128]{3,2,1,0:T(8,128)(2,1)S(1)}, u32[]{:S(2)}) %copy-start.2) | copy-done | bytes 7864344
  45.1 3.7 slice.103
  48.8 14.0 %copy.36 = bf16[20,128,12,128]{1,3,2,0:T(8,128)(2,1)} copy(bf16[20,128,12,128]{3,2,1,0:T(8,128)(2,1)} %copy-done.2) | data formatting | bytes 15728640 | tf_op jit(solution)/shard_map/convert_element_type | solution.py:41
  62.9 8.6 %copy.34 = bf16[12,128,12,128]{1,3,2,0:T(8,128)(2,1)} copy(bf16[12,128,12,128]{3,2,1,0:T(8,128)(2,1)} %slice.103) | data formatting | bytes 9437184 | tf_op jit(solution)/shard_map/slice | solution.py:69
  71.4 6.7 %gather_fusion.6 = bf16[12,128,1536]{1,2,0:T(8,128)(2,1)} fusion(bf16[20,128,1536]{1,2,0:T(8,128)(2,1)} %bitcast.81, s32[1024]{0:T(1024)S(1)} %get-tuple-element.37), kind=kCustom, calls=%fused_computation.6.clone | custom fusion | bytes 9437232 | tf_op jit(solution)/shard_map/jit(_take)/gather | solution.py:64
  78.1 6.6 %gather_fusion.5 = bf16[12,128,1536]{1,2,0:T(8,128)(2,1)} fusion(bf16[20,128,1536]{1,2,0:T(8,128)(2,1)} %bitcast.82, s32[1024]{0:T(1024)S(1)} %get-tuple-element.38), kind=kCustom, calls=%fused_computation.5.clone | custom fusion | bytes 9437232 | tf_op jit(solution)/shard_map/jit(_take)/gather | solution.py:64
  84.7 6.7 %gather_fusion.4 = bf16[12,128,1536]{1,2,0:T(8,128)(2,1)} fusion(bf16[20,128,1536]{1,2,0:T(8,128)(2,1)} %bitcast.83, s32[1024]{0:T(1024)S(1)} %get-tuple-element.39), kind=kCustom, calls=%fused_computation.4.clone | custom fusion | bytes 9437232 | tf_op jit(solution)/shard_map/jit(_take)/gather | solution.py:64
  91.4 6.8 %gather_fusion.3 = bf16[12,128,1536]{1,2,0:T(8,128)(2,1)} fusion(bf16[20,128,1536]{1,2,0:T(8,128)(2,1)} %bitcast.84, s32[1024]{0:T(1024)S(1)} %get-tuple-element.40), kind=kCustom, calls=%fused_computation.3.clone | custom fusion | bytes 9437232 | tf_op jit(solution)/shard_map/jit(_take)/gather | solution.py:64
  98.2 6.7 %gather_fusion.2 = bf16[12,128,1536]{1,2,0:T(8,128)(2,1)} fusion(bf16[20,128,1536]{1,2,0:T(8,128)(2,1)} %bitcast.85, s32[1024]{0:T(1024)S(1)} %get-tuple-element.41), kind=kCustom, calls=%fused_computation.2.clone | custom fusion | bytes 9437232 | tf_op jit(solution)/shard_map/jit(_take)/gather | solution.py:64
  104.8 6.7 %gather_fusion.1 = bf16[12,128,1536]{1,2,0:T(8,128)(2,1)} fusion(bf16[20,128,1536]{1,2,0:T(8,128)(2,1)} %bitcast.86, s32[1024]{0:T(1024)S(1)} %get-tuple-element.42), kind=kCustom, calls=%fused_computation.1.clone | custom fusion | bytes 9437232 | tf_op jit(solution)/shard_map/jit(_take)/gather | solution.py:64
  111.5 0.0 copy-start.3
  111.5 6.8 %gather_fusion = bf16[12,128,1536]{1,2,0:T(8,128)(2,1)} fusion(bf16[20,128,1536]{1,2,0:T(8,128)(2,1)} %bitcast.87, s32[1024]{0:T(1024)S(1)} %pad_clamp_fusion.6), kind=kCustom, calls=%fused_computation.clone | custom fusion | bytes 9437232 | tf_op jit(solution)/shard_map/jit(_take)/gather | solution.py:64
  118.3 0.0 copy-done.3
  118.3 7.6 %fusion.13 = f32[12,1536,128]{2,1,0:T(8,128)} fusion(bf16[12,128,1536]{1,2,0:T(8,128)(2,1)} %gather_fusion, pred[12]{0:T(512)(128)(4,1)S(1)} %get-tuple-element.35, bf16[1,12,7,128,128]{4,3,2,1,0:T(8,128)(2,1)S(1)} %copy-done.3), kind=kOutput, calls=%fused_computation.23 | convolution fusion | flops 606339072 | bytes 14549504 | tf_op jit(solution)/shard_map/rab,rbw->raw/dot_general | solution.py:65
  125.9 0.0 slice-done.8
  125.9 0.0 slice-done.9
  125.9 0.0 slice-start.4
  125.9 4.5 %fusion.11 = f32[12,1536,128]{2,1,0:T(8,128)} fusion(bf16[12,128,1536]{1,2,0:T(8,128)(2,1)S(1)} %bitcast.98, pred[12]{0:T(512)(128)(4,1)S(1)} %get-tuple-element.33, bf16[1,12,7,128,128]{4,3,2,1,0:T(8,128)(2,1)S(1)} %copy-done.3), kind=kOutput, calls=%fused_computation.21 | convolution fusion | flops 606339072 | bytes 14549504 | tf_op jit(solution)/shard_map/rab,rbw->raw/dot_general | solution.py:65
  130.4 0.0 slice-done.6
  130.4 0.0 slice-done.7
  130.4 0.0 slice-start.2
  130.4 4.7 %fusion.9 = f32[12,1536,128]{2,1,0:T(8,128)} fusion(bf16[12,128,1536]{1,2,0:T(8,128)(2,1)S(1)} %bitcast.96, pred[12]{0:T(512)(128)(4,1)S(1)} %get-tuple-element.31, bf16[1,12,7,128,128]{4,3,2,1,0:T(8,128)(2,1)S(1)} %copy-done.3), kind=kOutput, calls=%fused_computation.19 | convolution fusion | flops 606339072 | bytes 14549504 | tf_op jit(solution)/shard_map/rab,rbw->raw/dot_general | solution.py:65
  135.2 0.0 slice-done.4
  135.2 0.0 slice-done.5
  135.2 0.0 slice-start
  135.2 4.5 %fusion.7 = f32[12,1536,128]{2,1,0:T(8,128)} fusion(bf16[12,128,1536]{1,2,0:T(8,128)(2,1)S(1)} %bitcast.94, pred[12]{0:T(512)(128)(4,1)S(1)} %get-tuple-element.29, bf16[1,12,7,128,128]{4,3,2,1,0:T(8,128)(2,1)S(1)} %copy-done.3), kind=kOutput, calls=%fused_computation.17 | convolution fusion | flops 606339072 | bytes 14549504 | tf_op jit(solution)/shard_map/rab,rbw->raw/dot_general | solution.py:65
  139.7 0.0 slice-done.2
  139.7 0.0 slice-done.3
  139.7 4.5 %fusion.5 = f32[12,1536,128]{2,1,0:T(8,128)} fusion(bf16[12,128,1536]{1,2,0:T(8,128)(2,1)S(1)} %bitcast.92, pred[12]{0:T(512)(128)(4,1)S(1)} %get-tuple-element.27, bf16[1,12,7,128,128]{4,3,2,1,0:T(8,128)(2,1)S(1)} %copy-done.3), kind=kOutput, calls=%fused_computation.15 | convolution fusion | flops 606339072 | bytes 14549504 | tf_op jit(solution)/shard_map/rab,rbw->raw/dot_general | solution.py:65
  144.2 0.0 slice-done
  144.2 0.0 slice-done.1
  144.2 4.4 %fusion.3 = f32[12,1536,128]{2,1,0:T(8,128)} fusion(bf16[12,128,1536]{1,2,0:T(8,128)(2,1)S(1)} %bitcast.90, pred[12]{0:T(512)(128)(4,1)S(1)} %get-tuple-element.25, bf16[1,12,7,128,128]{4,3,2,1,0:T(8,128)(2,1)S(1)} %copy-done.3), kind=kOutput, calls=%fused_computation.13 | convolution fusion | flops 606339072 | bytes 14549504 | tf_op jit(solution)/shard_map/rab,rbw->raw/dot_general | solution.py:65
  148.6 27.6 %convolution_bitcast_fusion = f32[1536,1536]{1,0:T(8,128)} fusion(bf16[12,128,1536]{1,2,0:T(8,128)(2,1)} %bitcast.99, f32[12,1536,128]{2,1,0:T(8,128)} %fusion.3, f32[12,1536,128]{2,1,0:T(8,128)} %fusion.5, f32[12,1536,128]{2,1,0:T(8,128)} %fusion.7, f32[12,1536,128]{2,1,0:T(8,128)} %fusion.9, f32[12,1536,128]{2,1,0:T(8,128)} %fusion.13, ...), kind=kOutput, calls=%fused_computation.9 | convolution fusion | flops 7870611456 | bytes 75891200 | tf_op jit(solution)/shard_map/dot_general | solution.py:70
  176.2 4.6 %fusion.68 = (f32[512,1536]{1,0:T(8,128)S(1)}, f32[512,1536]{1,0:T(8,128)S(1)}, f32[512,1536]{1,0:T(8,128)S(1)}) fusion(f32[1536,1536]{1,0:T(8,128)} %convolution_bitcast_fusion), kind=kLoop, calls=%fused_computation.106 | loop fusion | bytes 18874368 | tf_op jit(solution)/shard_map/slice | solution.py:80
  180.8 1.3 collective-permute-start.3
  182.1 5.2 %collective-permute-start.2 = (f32[512,1536]{1,0:T(8,128)S(1)}, f32[512,1536]{1,0:T(8,128)S(1)}, u32[]{:S(2)}, u32[]{:S(2)}) collective-permute-start(f32[512,1536]{1,0:T(8,128)S(1)} %get-tuple-element.22), channel_id=1, source_target_pairs={{0,4},{4,8},{8,12},{12,16},{16,20},{20,24},{24,28},{1,5},{5,9},{9,... | collective-permute-start | bytes 9437192 | tf_op jit(solution)/shard_map/ppermute | solution.py:25
  187.3 65.1 %collective-permute-done.3 = f32[512,1536]{1,0:T(8,128)S(1)} collective-permute-done((f32[512,1536]{1,0:T(8,128)S(1)}, f32[512,1536]{1,0:T(8,128)S(1)}, u32[]{:S(2)}, u32[]{:S(2)}) %collective-permute-start.3) | collective-permute-done | bytes 3145760 | tf_op jit(solution)/shard_map/ppermute | solution.py:25
  252.4 68.5 %collective-permute-done.2 = f32[512,1536]{1,0:T(8,128)S(1)} collective-permute-done((f32[512,1536]{1,0:T(8,128)S(1)}, f32[512,1536]{1,0:T(8,128)S(1)}, u32[]{:S(2)}, u32[]{:S(2)}) %collective-permute-start.2) | collective-permute-done | bytes 3145760 | tf_op jit(solution)/shard_map/ppermute | solution.py:25
  320.9 3.2 pad_add_fusion
  324.1 0.0 reduce-scatter.2.cloned.1.call-update
  324.1 53.0 %reduce-scatter.2.cloned.1.call-done = f32[1,128,2560]{2,1,0:T(8,128)} async-done(((f32[4,128,2560]{2,1,0:T(8,128)}), f32[1,128,2560]{2,1,0:T(8,128)}) %reduce-scatter.2.cloned.1.call-update) | async-done | bytes 1310736 | tf_op jit(solution)/shard_map/reduce_scatter | solution.py:84
  377.1 0.0 copy-done.1
  (20 shorter events, 0.1 us)
Async XLA Ops:
  6.5 9.6 %copy-start = (s32[4,96,4]{1,2,0:T(4,128)S(1)}, s32[4,96,4]{1,2,0:T(4,128)}, u32[]{:S(2)}) copy-start(s32[4,96,4]{1,2,0:T(4,128)} %param.10) | copy-start | bytes 18436
  6.5 9.3 %copy-start.5 = (s32[8,4]{0,1:T(4,128)S(1)}, s32[8,4]{0,1:T(4,128)}, u32[]{:S(2)}) copy-start(s32[8,4]{0,1:T(4,128)} %param.11) | copy-start | bytes 388
  6.5 9.6 %copy-start.4 = (s32[1,12,7]{1,0,2:T(1,128)S(1)}, s32[1,12,7]{1,0,2:T(1,128)}, u32[]{:S(2)}) copy-start(s32[1,12,7]{1,0,2:T(1,128)} %param.8) | copy-start | bytes 1012
  6.5 370.6 %reduce-scatter.2.cloned.1.call-start = ((), (), s32[]{:S(2)}) async-start(), calls=%async_computation.1 | async-start | bytes 6553600 | tf_op jit(solution)/shard_map/reduce_scatter | solution.py:84
  9.6 27.3 %collective-permute-start = (bf16[1,4,4,128,128]{4,2,3,1,0:T(4,128)(2,1)S(1)}, bf16[1,4,4,128,128]{4,2,3,1,0:T(4,128)(2,1)S(1)}, u32[]{:S(2)}, u32[]{:S(2)}) collective-permute-start(bf16[1,4,4,128,128]{4,2,3,1,0:T(4,128)(2,1)S(1)} %get-tuple-element.23), channel_id=1, source_target_pairs={{0,4},{4,8},{8,12},{12,16},{16,20},{20,24},{24,28},{1,5},{5,9},{9,... | collective-permute-start | bytes 1572872 | tf_op jit(solution)/shard_map/ppermute | solution.py:16
  14.5 22.4 %collective-permute-start.1 = (bf16[1,4,4,128,128]{4,2,3,1,0:T(4,128)(2,1)S(1)}, bf16[1,4,4,128,128]{4,2,3,1,0:T(4,128)(2,1)}, u32[]{:S(2)}, u32[]{:S(2)}) collective-permute-start(bf16[1,4,4,128,128]{4,2,3,1,0:T(4,128)(2,1)S(1)} %get-tuple-element.24), channel_id=1, source_target_pairs={{4,0},{8,4},{12,8},{16,12},{20,16},{24,20},{28,24},{5,1},{9,5},{13... | collective-permute-start | bytes 1572872 | tf_op jit(solution)/shard_map/ppermute | solution.py:17
  41.1 4.0 %copy-start.2 = (bf16[20,128,12,128]{3,2,1,0:T(8,128)(2,1)}, bf16[20,128,12,128]{3,2,1,0:T(8,128)(2,1)S(1)}, u32[]{:S(2)}) copy-start(bf16[20,128,12,128]{3,2,1,0:T(8,128)(2,1)S(1)} %convert_bitcast_fusion) | copy-start | bytes 23592964
  111.5 6.8 %copy-start.3 = (bf16[1,12,7,128,128]{4,3,2,1,0:T(8,128)(2,1)S(1)}, bf16[1,12,7,128,128]{4,3,2,1,0:T(8,128)(2,1)}, u32[]{:S(2)}) copy-start(bf16[1,12,7,128,128]{4,3,2,1,0:T(8,128)(2,1)} %param.7) | copy-start | bytes 8257540
  111.5 14.4 %slice-start.8 = ((s8[4718592]{0:T(1024)(128)(4,1)}), s8[524288]{0:T(1024)(128)(4,1)S(1)}, s32[]{:S(2)}) async-start(s8[4718592]{0:T(1024)(128)(4,1)} %bitcast.97), calls=%async_computation.10 | async-start | bytes 1048576
  118.3 7.6 %slice-start.9 = ((s8[4718592]{0:T(1024)(128)(4,1)}), s8[4194304]{0:T(1024)(128)(4,1)S(1)}, s32[]{:S(2)}) async-start(s8[4718592]{0:T(1024)(128)(4,1)} %bitcast.97), calls=%async_computation.11 | async-start | bytes 8388608
  118.3 12.1 %slice-start.6 = ((s8[4718592]{0:T(1024)(128)(4,1)}), s8[4194304]{0:T(1024)(128)(4,1)S(1)}, s32[]{:S(2)}) async-start(s8[4718592]{0:T(1024)(128)(4,1)} %bitcast.95), calls=%async_computation.8 | async-start | bytes 8388608
  125.9 4.5 %slice-start.7 = ((s8[4718592]{0:T(1024)(128)(4,1)}), s8[524288]{0:T(1024)(128)(4,1)S(1)}, s32[]{:S(2)}) async-start(s8[4718592]{0:T(1024)(128)(4,1)} %bitcast.95), calls=%async_computation.9 | async-start | bytes 1048576
  125.9 9.3 %slice-start.4 = ((s8[4718592]{0:T(1024)(128)(4,1)}), s8[4194304]{0:T(1024)(128)(4,1)S(1)}, s32[]{:S(2)}) async-start(s8[4718592]{0:T(1024)(128)(4,1)} %bitcast.93), calls=%async_computation.6 | async-start | bytes 8388608
  130.4 4.8 %slice-start.5 = ((s8[4718592]{0:T(1024)(128)(4,1)}), s8[524288]{0:T(1024)(128)(4,1)S(1)}, s32[]{:S(2)}) async-start(s8[4718592]{0:T(1024)(128)(4,1)} %bitcast.93), calls=%async_computation.7 | async-start | bytes 1048576
  130.4 9.3 %slice-start.2 = ((s8[4718592]{0:T(1024)(128)(4,1)}), s8[4194304]{0:T(1024)(128)(4,1)S(1)}, s32[]{:S(2)}) async-start(s8[4718592]{0:T(1024)(128)(4,1)} %bitcast.91), calls=%async_computation.4 | async-start | bytes 8388608
  135.2 4.5 %slice-start.3 = ((s8[4718592]{0:T(1024)(128)(4,1)}), s8[524288]{0:T(1024)(128)(4,1)S(1)}, s32[]{:S(2)}) async-start(s8[4718592]{0:T(1024)(128)(4,1)} %bitcast.91), calls=%async_computation.5 | async-start | bytes 1048576
  135.2 9.0 %slice-start = ((s8[4718592]{0:T(1024)(128)(4,1)}), s8[4194304]{0:T(1024)(128)(4,1)S(1)}, s32[]{:S(2)}) async-start(s8[4718592]{0:T(1024)(128)(4,1)} %bitcast.89), calls=%async_computation.2 | async-start | bytes 8388608
  139.7 4.5 %slice-start.1 = ((s8[4718592]{0:T(1024)(128)(4,1)}), s8[524288]{0:T(1024)(128)(4,1)S(1)}, s32[]{:S(2)}) async-start(s8[4718592]{0:T(1024)(128)(4,1)} %bitcast.89), calls=%async_computation.3 | async-start | bytes 1048576
  180.8 71.6 %collective-permute-start.3 = (f32[512,1536]{1,0:T(8,128)S(1)}, f32[512,1536]{1,0:T(8,128)S(1)}, u32[]{:S(2)}, u32[]{:S(2)}) collective-permute-start(f32[512,1536]{1,0:T(8,128)S(1)} %get-tuple-element.21), channel_id=1, source_target_pairs={{4,0},{8,4},{12,8},{16,12},{20,16},{24,20},{28,24},{5,1},{9,5},{13... | collective-permute-start | bytes 9437192 | tf_op jit(solution)/shard_map/ppermute | solution.py:25
  182.1 138.8 %collective-permute-start.2 = (f32[512,1536]{1,0:T(8,128)S(1)}, f32[512,1536]{1,0:T(8,128)S(1)}, u32[]{:S(2)}, u32[]{:S(2)}) collective-permute-start(f32[512,1536]{1,0:T(8,128)S(1)} %get-tuple-element.22), channel_id=1, source_target_pairs={{0,4},{4,8},{8,12},{12,16},{16,20},{20,24},{24,28},{1,5},{5,9},{9,... | collective-permute-start | bytes 9437192 | tf_op jit(solution)/shard_map/ppermute | solution.py:25
  320.9 56.2 %copy-start.1 = (s32[4,96,4]{1,2,0:T(4,128)S(1)}, s32[4,96,4]{1,2,0:T(4,128)}, u32[]{:S(2)}) copy-start(s32[4,96,4]{1,2,0:T(4,128)} %param.10) | copy-start | bytes 18436
Sparse Core Ops, SparseCore 0:
  324.2 52.8 reduce-scatter.1
where the time goes:
time: 385 us; the launch traced here: 384 us
  waiting for transfers between devices  207 us (54%)
  local copies, waits for them, and re-layouts  85.2 us (22%)
  matrix products  62.1 us (16%)
  between operations  13.6 us (4%)
  starting transfers between devices  12.7 us (3%)
    ppermute x2, waiting for transfers between devices, passed_along(): return lax.ppermute(shard, axis, pairs)  134 us
    reduce_scatter x1, waiting for transfers between devices, on_device(): result = lax.psum_scatter(full, 'plane', scatter_dimension=0, tiled=True)  53 us
    gather x7, local copies, waits for them, and re-layouts, on_device(): picked = jnp.take(dense, local[:, k], axis=0)  46.9 us
    dot_general x6, matrix products, on_device(): jnp.einsum('rab,rbw->raw', a_blocks[0, :, k], picked, preferred_element_t...  30.2 us
    dot_general x1, matrix products, on_device(): lax.dot_general(own_rows, product.reshape(-1, width), (((0,), (0,)), ((),...  27.6 us
    ppermute x1, waiting for transfers between devices, with_halo(): before = lax.ppermute(last, axis, up)  20.3 us
    convert_element_type x1, local copies, waits for them, and re-layouts, window_rows(): return dense.reshape(count, block, 3 * coarse * block).astype(jnp.bfloat16)  14 us
    slice x2, local copies, waits for them, and re-layouts, on_device(): own_rows = dense[GHOST:GHOST + rows_here].reshape(-1, width)  12.2 us
  transfers between devices with their start and end apart: 5, of which 4 were waited for; matrix products, arithmetic and copies ran while one was open for 0% of the time, Pallas kernels for 0%

commit v1 on v0

v1 whole, which is shorter than its diff:
```python
import functools

import jax
import jax.numpy as jnp
from jax import lax
from jax.experimental import pallas as pl
from jax.experimental.pallas import tpu as pltpu
from jax.sharding import PartitionSpec as P

GHOST = 4
MESH = pl.DeviceIdType.MESH


def kernel(dims, table, picks, a_hbm, p_hbm, out, *scratch):
    slabs, planes, rows, links, kp, block, coarse, owned = dims
    stages = planes.bit_length() - 1
    edge = coarse * block
    width = 3 * edge
    chunks = 3
    (a_own, p_own, p_low, p_high, pt, q, qt0, qt1, qt2, ap, final,
     send_c, recv_c, local_sem, halo_send, halo_recv, c_sem, c_got) = scratch[:18]
    rest = scratch[18:]
    send_b, recv_b, keep_b, b_sem, b_got = (rest[i * stages : (i + 1) * stages] for i in range(5))
    slab = lax.axis_index("slab")
    me = lax.axis_index("plane")
    bits = [(me // (1 << t)) % 2 for t in range(stages)]
    partners = [me + (1 - 2 * bits[t]) * (1 << t) for t in range(stages)]
    has_low = slab > 0
    has_high = slab < slabs - 1

    copy_a = pltpu.make_async_copy(a_hbm, a_own, local_sem.at[0])
    copy_p = pltpu.make_async_copy(p_hbm, p_own.at[pl.ds(0, rows * kp)], local_sem.at[1])
    copy_p.start()
    copy_a.start()

    barrier = pltpu.get_barrier_semaphore()
    for t in range(stages):
        pl.semaphore_signal(barrier, inc=1, device_id=(slab, partners[t]), device_id_type=MESH)

    @pl.when(has_low)
    def _():
        pl.semaphore_signal(barrier, inc=1, device_id=(slab - 1, me), device_id_type=MESH)

    @pl.when(has_high)
    def _():
        pl.semaphore_signal(barrier, inc=1, device_id=(slab + 1, me), device_id_type=MESH)

    neighbours = stages + jnp.where(has_low, 1, 0) + jnp.where(has_high, 1, 0)
    pl.semaphore_wait(barrier, neighbours)

    ghosts = GHOST * kp
    halo_up = pltpu.make_async_remote_copy(
        src_ref=p_hbm.at[pl.ds((rows - GHOST) * kp, ghosts)],
        dst_ref=p_low.at[pl.ds(0, ghosts)],
        send_sem=halo_send.at[0], recv_sem=halo_recv.at[0],
        device_id=(slab + 1, me), device_id_type=MESH)
    halo_down = pltpu.make_async_remote_copy(
        src_ref=p_hbm.at[pl.ds(0, ghosts)],
        dst_ref=p_high.at[pl.ds(0, ghosts)],
        send_sem=halo_send.at[1], recv_sem=halo_recv.at[1],
        device_id=(slab - 1, me), device_id_type=MESH)

    @pl.when(has_high)
    def _():
        halo_up.start()

    @pl.when(has_low)
    def _():
        halo_down.start()

    zero = jnp.zeros((block, block), jnp.bfloat16)
    p_own[rows * kp] = zero
    p_low[ghosts] = zero
    p_high[ghosts] = zero

    @pl.when(slab == 0)
    def _():
        p_low[...] = jnp.zeros_like(p_low)
        recv_c[1] = jnp.zeros(recv_c.shape[1:], recv_c.dtype)

    @pl.when(slab == slabs - 1)
    def _():
        p_high[...] = jnp.zeros_like(p_high)
        recv_c[0] = jnp.zeros(recv_c.shape[1:], recv_c.dtype)

    def spread(first, count, blocks):
        def body(i, _):
            n = first + i
            for w in range(3 * coarse):
                q[n, :, w * block : (w + 1) * block] = blocks[table[n, w]]
            return 0

        lax.fori_loop(0, count, body, 0)

    def multiply(first, count):
        def body(i, _):
            g = first + i
            left = jnp.concatenate([a_own[g * links + k] for k in range(links)], axis=1)
            at = [picks[g, k] for k in range(links)]
            for c in range(chunks):
                right = jnp.concatenate(
                    [q[at[k], :, c * edge : (c + 1) * edge] for k in range(links)], axis=0)
                ap[pl.ds(pl.multiple_of(g * block, block), block), c * edge : (c + 1) * edge] = jnp.dot(
                    left, right, preferred_element_type=jnp.float32).astype(jnp.bfloat16)
            return 0

        lax.fori_loop(0, count, body, 0)

    copy_p.wait()
    spread(GHOST, rows, p_own)

    def flip(b, _):
        pt[b] = p_own[b].T
        return 0

    lax.fori_loop(0, rows * kp + 1, flip, 0)
    parts = ((qt0, 0, GHOST), (qt1, 0, rows), (qt2, rows - GHOST, GHOST))
    for j, (qt, first, count) in enumerate(parts):
        for i in range(count):
            for slot in range(coarse):
                qt[slot // owned, (slot % owned) * block : (slot % owned + 1) * block, i * block : (i + 1) * block] = (
                    pt[table[GHOST + first + i, j * coarse + slot]])
    copy_a.wait()
    multiply(GHOST, rows - 2 * GHOST)

    def stage_copy(t, j, c):
        return pltpu.make_async_remote_copy(
            src_ref=send_b[t].at[j, c], dst_ref=recv_b[t].at[j, c],
            send_sem=b_sem[t].at[j, c], recv_sem=b_got[t].at[j, c],
            device_id=(slab, partners[t]), device_id_type=MESH)

    def final_copy(j, c):
        return pltpu.make_async_remote_copy(
            src_ref=send_c.at[j, c], dst_ref=recv_c.at[j, c],
            send_sem=c_sem.at[j, c], recv_sem=c_got.at[j, c],
            device_id=(slab - 1 if j == 0 else slab + 1, me), device_id_type=MESH)

    def form(j):
        qt, first, count = parts[j]
        half = planes // 2
        for c in range(chunks):
            right = ap[first * block : (first + count) * block, c * edge : (c + 1) * edge]
            for i in range(half):
                send_b[0][j, c, i] = jnp.dot(
                    qt[1 - bits[0] + 2 * i], right, preferred_element_type=jnp.float32).astype(jnp.bfloat16)
            stage_copy(0, j, c).start()
            for i in range(half):
                keep_b[0][j, c, i] = jnp.dot(
                    qt[bits[0] + 2 * i], right, preferred_element_type=jnp.float32)

    def fold(t, j):
        for c in range(chunks):
            stage_copy(t - 1, j, c).wait_recv()
            for i in range(planes >> (t + 1)):
                at = 1 - bits[t] + 2 * i
                send_b[t][j, c, i] = (
                    keep_b[t - 1][j, c, at] + recv_b[t - 1][j, c, at].astype(jnp.float32)).astype(jnp.bfloat16)
            stage_copy(t, j, c).start()
            for i in range(planes >> (t + 1)):
                at = bits[t] + 2 * i
                keep_b[t][j, c, i] = keep_b[t - 1][j, c, at] + recv_b[t - 1][j, c, at].astype(jnp.float32)

    def finish(j):
        for c in range(chunks):
            stage_copy(stages - 1, j, c).wait_recv()
            value = keep_b[stages - 1][j, c, 0] + recv_b[stages - 1][j, c, 0].astype(jnp.float32)
            if j == 1:
                final[c] = value
            else:
                send_c[j // 2, c] = value.astype(jnp.bfloat16)

                @pl.when(has_low if j == 0 else has_high)
                def _():
                    final_copy(j // 2, c).start()

    @pl.when(has_low)
    def _():
        halo_up.wait_recv()

    spread(0, GHOST, p_low)
    multiply(0, GHOST)
    form(0)
    for t in range(1, stages):
        fold(t, 0)

    @pl.when(has_high)
    def _():
        halo_down.wait_recv()

    spread(GHOST + rows, GHOST, p_high)
    multiply(rows - GHOST, GHOST)
    form(2)
    finish(0)
    for t in range(1, stages):
        fold(t, 2)
    form(1)
    finish(2)
    for t in range(1, stages):
        fold(t, 1)
    finish(1)

    @pl.when(has_high)
    def _():
        for c in range(chunks):
            final_copy(0, c).wait_recv()

    @pl.when(has_low)
    def _():
        for c in range(chunks):
            final_copy(1, c).wait_recv()

    for o in range(5):
        terms = []
        if 0 <= o - 1 < chunks:
            terms.append(final[o - 1])
        if o < chunks:
            terms.append(recv_c[1, o].astype(jnp.float32))
        if o >= 2:
            terms.append(recv_c[0, o - 2].astype(jnp.float32))
        out[:, o * edge : (o + 1) * edge] = functools.reduce(jnp.add, terms)

    @pl.when(has_high)
    def _():
        halo_up.wait_send()
        for c in range(chunks):
            final_copy(1, c).wait_send()

    @pl.when(has_low)
    def _():
        halo_down.wait_send()
        for c in range(chunks):
            final_copy(0, c).wait_send()

    for t in range(stages):
        for j in range(3):
            for c in range(chunks):
                stage_copy(t, j, c).wait_send()


def tables(a_cols, p_cols, coarse_slot, rows, coarse):
    slab = lax.axis_index("slab")
    column = lax.axis_index("plane")
    start = slab * rows
    kp = p_cols.shape[2]
    mine = lax.dynamic_slice_in_dim(p_cols, column, 1, 0)[0]
    mine = jnp.pad(mine, ((GHOST, GHOST), (0, 0)))
    cols = lax.dynamic_slice_in_dim(mine, start, rows + 2 * GHOST, 0)
    slots = jnp.pad(coarse_slot, ((1, 1), (0, 0)))
    nearby = lax.dynamic_slice_in_dim(slots, slab, 3, 0).reshape(-1)
    relative = cols - (slab - 1) * coarse
    lanes = jnp.arange(3 * coarse, dtype=jnp.int32)
    slot = jnp.sum(jnp.where(relative[:, :, None] == lanes, nearby, 0), axis=-1)
    place = relative // coarse * coarse + slot
    match = place[:, :, None] == lanes
    which = jnp.max(jnp.where(match, jnp.arange(kp, dtype=jnp.int32)[None, :, None], -1), axis=1)
    n = jnp.arange(rows + 2 * GHOST, dtype=jnp.int32)
    low, high = n < GHOST, n >= GHOST + rows
    base = jnp.where(low, n, jnp.where(high, n - GHOST - rows, n - GHOST)) * kp
    none = jnp.where(low | high, GHOST * kp, rows * kp)
    table = jnp.where(which >= 0, base[:, None] + which, none[:, None])
    return table, a_cols[0] - (start - GHOST)


def on_device(a_blocks, a_cols, p_blocks, p_cols, coarse_slot):
    rows, links, block = a_blocks.shape[1:4]
    kp = p_blocks.shape[2]
    coarse = coarse_slot.shape[1]
    slabs = lax.axis_size("slab")
    planes = lax.axis_size("plane")
    owned = coarse // planes
    stages = planes.bit_length() - 1
    assert planes == 1 << stages and stages > 0
    edge = coarse * block
    width = 3 * edge
    high = owned * block
    table, picks = tables(a_cols, p_cols, coarse_slot, rows, coarse)
    dims = (slabs, planes, rows, links, kp, block, coarse, owned)
    bf, f32 = jnp.bfloat16, jnp.float32
    vmem = pltpu.VMEM
    dma = pltpu.SemaphoreType.DMA
    shape = lambda t: (3, 3, planes >> (t + 1), high, edge)
    scratch = [
        vmem((rows * links, block, block), bf),
        vmem((rows * kp + 1, block, block), bf),
        vmem((GHOST * kp + 1, block, block), bf),
        vmem((GHOST * kp + 1, block, block), bf),
        vmem((rows * kp + 1, block, block), bf),
        vmem((rows + 2 * GHOST, block, width), bf),
        vmem((planes, high, GHOST * block), bf),
        vmem((planes, high, rows * block), bf),
        vmem((planes, high, GHOST * block), bf),
        vmem((rows * block, width), bf),
        vmem((3, high, edge), f32),
        vmem((2, 3, high, edge), bf),
        vmem((2, 3, high, edge), bf),
        dma((2,)), dma((2,)), dma((2,)), dma((2, 3)), dma((2, 3)),
    ]
    scratch += [vmem(shape(t), bf) for t in range(stages)]
    scratch += [vmem(shape(t), bf) for t in range(stages)]
    scratch += [vmem(shape(t), f32) for t in range(stages)]
    scratch += [dma((3, 3)) for t in range(2 * stages)]
    smem = pl.BlockSpec(memory_space=pltpu.SMEM)
    anywhere = pl.BlockSpec(memory_space=pl.ANY)
    result = pl.pallas_call(
        functools.partial(kernel, dims),
        out_shape=jax.ShapeDtypeStruct((high, 5 * edge), f32),
        in_specs=[smem, smem, anywhere, anywhere],
        out_specs=pl.BlockSpec(memory_space=pltpu.VMEM),
        scratch_shapes=scratch,
        compiler_params=pltpu.CompilerParams(
            collective_id=0, has_side_effects=True, vmem_limit_bytes=62 * 1024 * 1024),
    )(table, picks, a_blocks.reshape(rows * links, block, block), p_blocks.reshape(rows * kp, block, block))
    return result.reshape(1, owned, block, 5 * edge)


def solution(mesh):
    return jax.shard_map(
        on_device,
        mesh=mesh,
        in_specs=(
            P("plane", "slab", None, None, None),
            P("plane", "slab", None),
            P("plane", "slab", None, None, None),
            P(),
            P(),
        ),
        out_specs=P("plane", "slab", None, None),
        check_vma=False,
    )
```

time: 385 us -> 69.9 us (0.18)
  the two profiles are of different devices: /device:TPU:0 before, /device:TPU:20 now
where the time goes in v1:
time: 69.9 us; the launch traced here: 69.5 us
  Pallas kernels  62.9 us (90%)
  local copies, waits for them, and re-layouts  4.88 us (7%)
  other arithmetic  1.66 us (2%)
    pallas_call x1, Pallas kernels, on_device(): pl.pallas_call(functools.partial(kernel, dims), out_shape=jax.ShapeDtypeS...  62.9 us
    unnamed x3, local copies, waits for them, and re-layouts  3.16 us

profile of v1, /device:TPU:20, one launch (start us, length us, event | category | flops | bytes accessed | tf_op | source)
XLA Modules:
  0.0 69.5 jit_solution(4006474361901991677)
XLA Ops:
  0.0 0.0 copy-start
  0.0 0.7 copy-done
  0.7 0.8 %pad_dynamic-slice_fusion = s32[3,4]{0,1:T(4,128)S(1)} fusion(s32[]{:T(128)S(6)} %select_n.52, s32[8,4]{0,1:T(4,128)} %param.9), kind=kLoop, calls=%fused_computation.16 | loop fusion | bytes 180 | tf_op jit(solution)/shard_map/dynamic_slice | solution.py:249
  1.5 0.1 copy.22
  1.6 0.1 reshape.34
  1.6 0.1 dynamic-slice_subtract_fusion
  1.7 0.1 select_reduce_fusion.1
  1.8 0.1 fusion.3
  1.9 0.7 fusion
  2.6 0.7 copy.26.picks
  3.3 0.1 copy.23
  3.4 0.7 add_select_fusion.table
  4.1 62.9 %shard_map.55 = f32[128,2560]{1,0:T(8,128)} custom-call(s32[20,12]{1,0:T(8,128)} %add_select_fusion.table, s32[12,7]{1,0:T(8,128)} %copy.26.picks, bf16[84,128,128]{2,1,0:T(8,128)(2,1)} %bitcast.8, bf16[48,128,128]{2,1,0:T(8,128)(2,1)} %bitcast.9), custom_call_target="tpu_custom_call" | custom-call | tf_op jit(solution)/shard_map/pallas_call | solution.py:304
  67.0 2.5 %copy.31 = f32[1,1,128,2560]{3,2,1,0:T(8,128)} copy(f32[1,1,128,2560]{3,2,1,0:T(8,128)} %bitcast.7) | data formatting | bytes 2621440
  (3 shorter events, 0.0 us)
Async XLA Ops:
  0.0 0.7 %copy-start = (s32[4,96,4]{1,2,0:T(4,128)S(1)}, s32[4,96,4]{1,2,0:T(4,128)}, u32[]{:S(2)}) copy-start(s32[4,96,4]{1,2,0:T(4,128)} %param.8) | copy-start | bytes 18436

commit v2 on v1

--- a/solution.py
+++ b/solution.py
@@ -11,15 +11,15 @@
 MESH = pl.DeviceIdType.MESH
 
 
-def kernel(dims, table, picks, a_hbm, p_hbm, out, *scratch):
+def kernel(dims, a_cols, p_cols, slots, a_hbm, p_hbm, out, *scratch):
     slabs, planes, rows, links, kp, block, coarse, owned = dims
     stages = planes.bit_length() - 1
     edge = coarse * block
     width = 3 * edge
     chunks = 3
     (a_own, p_own, p_low, p_high, pt, q, qt0, qt1, qt2, ap, final,
-     send_c, recv_c, local_sem, halo_send, halo_recv, c_sem, c_got) = scratch[:18]
-    rest = scratch[18:]
+     send_c, recv_c, local_sem, halo_send, halo_recv, c_sem, c_got, table) = scratch[:19]
+    rest = scratch[19:]
     send_b, recv_b, keep_b, b_sem, b_got = (rest[i * stages : (i + 1) * stages] for i in range(5))
     slab = lax.axis_index("slab")
     me = lax.axis_index("plane")
@@ -64,9 +64,27 @@
     def _():
         halo_up.start()
 
-    @pl.when(has_low)
-    def _():
-        halo_down.start()
+    start = slab * rows
+    total = p_cols.shape[2]
+
+    def chart(n, _):
+        row = jnp.clip(start - GHOST + n, 0, total - 1)
+        place = []
+        for m in range(kp):
+            col = p_cols[me, m, row]
+            near = col // coarse
+            place.append((near - slab + 1) * coarse + slots[col % coarse, near])
+        low, high = n < GHOST, n >= GHOST + rows
+        base = jnp.where(low, n, jnp.where(high, n - GHOST - rows, n - GHOST)) * kp
+        none = jnp.where(low | high, GHOST * kp, rows * kp)
+        for w in range(3 * coarse):
+            value = none
+            for m in range(kp):
+                value = jnp.where(place[m] == w, base + m, value)
+            table[n, w] = value
+        return 0
+
+    lax.fori_loop(0, rows + 2 * GHOST, chart, 0)
 
     zero = jnp.zeros((block, block), jnp.bfloat16)
     p_own[rows * kp] = zero
@@ -96,7 +114,7 @@
         def body(i, _):
             g = first + i
             left = jnp.concatenate([a_own[g * links + k] for k in range(links)], axis=1)
-            at = [picks[g, k] for k in range(links)]
+            at = [jnp.clip(a_cols[k, 0, g] - (start - GHOST), 0, rows + 2 * GHOST - 1) for k in range(links)]
             for c in range(chunks):
                 right = jnp.concatenate(
                     [q[at[k], :, c * edge : (c + 1) * edge] for k in range(links)], axis=0)
@@ -160,8 +178,8 @@
                 at = bits[t] + 2 * i
                 keep_b[t][j, c, i] = keep_b[t - 1][j, c, at] + recv_b[t - 1][j, c, at].astype(jnp.float32)
 
-    def finish(j):
-        for c in range(chunks):
+    def finish(j, which):
+        for c in which:
             stage_copy(stages - 1, j, c).wait_recv()
             value = keep_b[stages - 1][j, c, 0] + recv_b[stages - 1][j, c, 0].astype(jnp.float32)
             if j == 1:
@@ -173,8 +191,13 @@
                 def _():
                     final_copy(j // 2, c).start()
 
+    @pl.when(has_high)
+    def _():
+        halo_up.wait_send()
+
     @pl.when(has_low)
     def _():
+        halo_down.start()
         halo_up.wait_recv()
 
     spread(0, GHOST, p_low)
@@ -182,6 +205,7 @@
     form(0)
     for t in range(1, stages):
         fold(t, 0)
+    finish(0, range(chunks - 1))
 
     @pl.when(has_high)
     def _():
@@ -189,15 +213,15 @@
 
     spread(GHOST + rows, GHOST, p_high)
     multiply(rows - GHOST, GHOST)
+    finish(0, range(chunks - 1, chunks))
     form(2)
-    finish(0)
     for t in range(1, stages):
         fold(t, 2)
     form(1)
-    finish(2)
     for t in range(1, stages):
         fold(t, 1)
-    finish(1)
+    finish(2, range(chunks))
+    finish(1, range(chunks))
 
     @pl.when(has_high)
     def _():
@@ -221,7 +245,6 @@
 
     @pl.when(has_high)
     def _():
-        halo_up.wait_send()
         for c in range(chunks):
             final_copy(1, c).wait_send()
 
@@ -235,30 +258,6 @@
         for j in range(3):
             for c in range(chunks):
                 stage_copy(t, j, c).wait_send()
-
-
-def tables(a_cols, p_cols, coarse_slot, rows, coarse):
-    slab = lax.axis_index("slab")
-    column = lax.axis_index("plane")
-    start = slab * rows
-    kp = p_cols.shape[2]
-    mine = lax.dynamic_slice_in_dim(p_cols, column, 1, 0)[0]
-    mine = jnp.pad(mine, ((GHOST, GHOST), (0, 0)))
-    cols = lax.dynamic_slice_in_dim(mine, start, rows + 2 * GHOST, 0)
-    slots = jnp.pad(coarse_slot, ((1, 1), (0, 0)))
-    nearby = lax.dynamic_slice_in_dim(slots, slab, 3, 0).reshape(-1)
-    relative = cols - (slab - 1) * coarse
-    lanes = jnp.arange(3 * coarse, dtype=jnp.int32)
-    slot = jnp.sum(jnp.where(relative[:, :, None] == lanes, nearby, 0), axis=-1)
-    place = relative // coarse * coarse + slot
-    match = place[:, :, None] == lanes
-    which = jnp.max(jnp.where(match, jnp.arange(kp, dtype=jnp.int32)[None, :, None], -1), axis=1)
-    n = jnp.arange(rows + 2 * GHOST, dtype=jnp.int32)
-    low, high = n < GHOST, n >= GHOST + rows
-    base = jnp.where(low, n, jnp.where(high, n - GHOST - rows, n - GHOST)) * kp
-    none = jnp.where(low | high, GHOST * kp, rows * kp)
-    table = jnp.where(which >= 0, base[:, None] + which, none[:, None])
-    return table, a_cols[0] - (start - GHOST)
 
 
 def on_device(a_blocks, a_cols, p_blocks, p_cols, coarse_slot):
@@ -273,7 +272,6 @@
     edge = coarse * block
     width = 3 * edge
     high = owned * block
-    table, picks = tables(a_cols, p_cols, coarse_slot, rows, coarse)
     dims = (slabs, planes, rows, links, kp, block, coarse, owned)
     bf, f32 = jnp.bfloat16, jnp.float32
     vmem = pltpu.VMEM
@@ -294,6 +292,7 @@
         vmem((2, 3, high, edge), bf),
         vmem((2, 3, high, edge), bf),
         dma((2,)), dma((2,)), dma((2,)), dma((2, 3)), dma((2, 3)),
+        pltpu.SMEM((rows + 2 * GHOST, 3 * coarse), jnp.int32),
     ]
     scratch += [vmem(shape(t), bf) for t in range(stages)]
     scratch += [vmem(shape(t), bf) for t in range(stages)]
@@ -304,12 +303,12 @@
     result = pl.pallas_call(
         functools.partial(kernel, dims),
         out_shape=jax.ShapeDtypeStruct((high, 5 * edge), f32),
-        in_specs=[smem, smem, anywhere, anywhere],
+        in_specs=[smem, smem, smem, anywhere, anywhere],
         out_specs=pl.BlockSpec(memory_space=pltpu.VMEM),
         scratch_shapes=scratch,
         compiler_params=pltpu.CompilerParams(
             collective_id=0, has_side_effects=True, vmem_limit_bytes=62 * 1024 * 1024),
-    )(table, picks, a_blocks.reshape(rows * links, block, block), p_blocks.reshape(rows * kp, block, block))
+    )(a_cols.transpose(2, 0, 1), p_cols.transpose(0, 2, 1), coarse_slot.T, a_blocks.reshape(rows * links, block, block), p_blocks.reshape(rows * kp, block, block))
     return result.reshape(1, owned, block, 5 * edge)
 
 

time: 69.9 us -> 57.3 us (0.82)
  the two profiles are of different devices: /device:TPU:20 before, /device:TPU:0 now
where the time goes in v2:
time: 57.3 us; the launch traced here: 57.1 us
  Pallas kernels  54.7 us (95%)
  local copies, waits for them, and re-layouts  2.47 us (4%)
    pallas_call x1, Pallas kernels, on_device(): pl.pallas_call(functools.partial(kernel, dims), out_shape=jax.ShapeDtypeS...  54.7 us
    unnamed x1, local copies, waits for them, and re-layouts  2.47 us

profile of v2, /device:TPU:0, one launch (start us, length us, event | category | flops | bytes accessed | tf_op | source)
XLA Modules:
  0.0 57.1 jit_solution(12614153663675869930)
XLA Ops:
  0.0 54.7 %shard_map.55 = f32[128,2560]{1,0:T(8,128)} custom-call(s32[7,1,12]{2,1,0:T(1,128)} %bitcast.10, s32[4,4,96]{2,1,0:T(4,128)} %bitcast.9, s32[4,8]{1,0:T(4,128)} %bitcast.11, bf16[84,128,128]{2,1,0:T(8,128)(2,1)} %bitcast.7, bf16[48,128,128]{2,1,0:T(8,128)(2,1)} %bitcast.8), custom_call_target="tpu_custom_call" | custom-call | tf_op jit(solution)/shard_map/pallas_call | solution.py:303
  54.7 2.5 %copy.7 = f32[1,1,128,2560]{3,2,1,0:T(8,128)} copy(f32[1,1,128,2560]{3,2,1,0:T(8,128)} %bitcast.6) | data formatting | bytes 2621440

commit v3 on v2

--- a/solution.py
+++ b/solution.py
@@ -11,15 +11,15 @@
 MESH = pl.DeviceIdType.MESH
 
 
-def kernel(dims, a_cols, p_cols, slots, a_hbm, p_hbm, out, *scratch):
+def kernel(dims, a_cols_hbm, p_cols_hbm, slots_hbm, a_hbm, p_hbm, out, *scratch):
     slabs, planes, rows, links, kp, block, coarse, owned = dims
     stages = planes.bit_length() - 1
     edge = coarse * block
     width = 3 * edge
     chunks = 3
     (a_own, p_own, p_low, p_high, pt, q, qt0, qt1, qt2, ap, final,
-     send_c, recv_c, local_sem, halo_send, halo_recv, c_sem, c_got, table) = scratch[:19]
-    rest = scratch[19:]
+     send_c, recv_c, local_sem, halo_send, halo_recv, c_sem, c_got, table, whole, out_sem, a_cols, p_cols, slots, index_sem) = scratch[:25]
+    rest = scratch[25:]
     send_b, recv_b, keep_b, b_sem, b_got = (rest[i * stages : (i + 1) * stages] for i in range(5))
     slab = lax.axis_index("slab")
     me = lax.axis_index("plane")
@@ -30,6 +30,13 @@
 
     copy_a = pltpu.make_async_copy(a_hbm, a_own, local_sem.at[0])
     copy_p = pltpu.make_async_copy(p_hbm, p_own.at[pl.ds(0, rows * kp)], local_sem.at[1])
+    copy_index = [
+        pltpu.make_async_copy(source, target, index_sem.at[i])
+        for i, (source, target) in enumerate(
+            ((a_cols_hbm, a_cols), (p_cols_hbm, p_cols), (slots_hbm, slots)))
+    ]
+    for copy in copy_index:
+        copy.start()
     copy_p.start()
     copy_a.start()
 
@@ -84,6 +91,8 @@
             table[n, w] = value
         return 0
 
+    for copy in copy_index:
+        copy.wait()
     lax.fori_loop(0, rows + 2 * GHOST, chart, 0)
 
     zero = jnp.zeros((block, block), jnp.bfloat16)
@@ -110,12 +119,12 @@
 
         lax.fori_loop(0, count, body, 0)
 
-    def multiply(first, count):
+    def multiply(first, count, columns):
         def body(i, _):
             g = first + i
             left = jnp.concatenate([a_own[g * links + k] for k in range(links)], axis=1)
             at = [jnp.clip(a_cols[k, 0, g] - (start - GHOST), 0, rows + 2 * GHOST - 1) for k in range(links)]
-            for c in range(chunks):
+            for c in columns:
                 right = jnp.concatenate(
                     [q[at[k], :, c * edge : (c + 1) * edge] for k in range(links)], axis=0)
                 ap[pl.ds(pl.multiple_of(g * block, block), block), c * edge : (c + 1) * edge] = jnp.dot(
@@ -139,7 +148,7 @@
                 qt[slot // owned, (slot % owned) * block : (slot % owned + 1) * block, i * block : (i + 1) * block] = (
                     pt[table[GHOST + first + i, j * coarse + slot]])
     copy_a.wait()
-    multiply(GHOST, rows - 2 * GHOST)
+    multiply(GHOST, rows - 2 * GHOST, range(chunks))
 
     def stage_copy(t, j, c):
         return pltpu.make_async_remote_copy(
@@ -153,10 +162,10 @@
             send_sem=c_sem.at[j, c], recv_sem=c_got.at[j, c],
             device_id=(slab - 1 if j == 0 else slab + 1, me), device_id_type=MESH)
 
-    def form(j):
+    def form(j, columns):
         qt, first, count = parts[j]
         half = planes // 2
-        for c in range(chunks):
+        for c in columns:
             right = ap[first * block : (first + count) * block, c * edge : (c + 1) * edge]
             for i in range(half):
                 send_b[0][j, c, i] = jnp.dot(
@@ -201,8 +210,9 @@
         halo_up.wait_recv()
 
     spread(0, GHOST, p_low)
-    multiply(0, GHOST)
-    form(0)
+    for c in range(chunks):
+        multiply(0, GHOST, (c,))
+        form(0, (c,))
     for t in range(1, stages):
         fold(t, 0)
     finish(0, range(chunks - 1))
@@ -212,12 +222,14 @@
         halo_down.wait_recv()
 
     spread(GHOST + rows, GHOST, p_high)
-    multiply(rows - GHOST, GHOST)
-    finish(0, range(chunks - 1, chunks))
-    form(2)
+    for c in range(chunks):
+        multiply(rows - GHOST, GHOST, (c,))
+        form(2, (c,))
+        if c == 0:
+            finish(0, range(chunks - 1, chunks))
     for t in range(1, stages):
         fold(t, 2)
-    form(1)
+    form(1, range(chunks))
     for t in range(1, stages):
         fold(t, 1)
     finish(2, range(chunks))
@@ -232,6 +244,9 @@
     def _():
         for c in range(chunks):
             final_copy(1, c).wait_recv()
+
+    def out_copy(o):
+        return pltpu.make_async_copy(whole.at[o], out.at[:, pl.ds(o * edge, edge)], out_sem.at[o])
 
     for o in range(5):
         terms = []
@@ -241,7 +256,8 @@
             terms.append(recv_c[1, o].astype(jnp.float32))
         if o >= 2:
             terms.append(recv_c[0, o - 2].astype(jnp.float32))
-        out[:, o * edge : (o + 1) * edge] = functools.reduce(jnp.add, terms)
+        whole[o] = functools.reduce(jnp.add, terms)
+        out_copy(o).start()
 
     @pl.when(has_high)
     def _():
@@ -258,6 +274,8 @@
         for j in range(3):
             for c in range(chunks):
                 stage_copy(t, j, c).wait_send()
+    for o in range(5):
+        out_copy(o).wait()
 
 
 def on_device(a_blocks, a_cols, p_blocks, p_cols, coarse_slot):
@@ -293,22 +311,30 @@
         vmem((2, 3, high, edge), bf),
         dma((2,)), dma((2,)), dma((2,)), dma((2, 3)), dma((2, 3)),
         pltpu.SMEM((rows + 2 * GHOST, 3 * coarse), jnp.int32),
+        vmem((5, high, edge), f32),
+        dma((5,)),
+        pltpu.SMEM((links, 1, rows), jnp.int32),
+        pltpu.SMEM((planes, kp, p_cols.shape[1]), jnp.int32),
+        pltpu.SMEM((coarse, slabs), jnp.int32),
+        dma((3,)),
     ]
     scratch += [vmem(shape(t), bf) for t in range(stages)]
     scratch += [vmem(shape(t), bf) for t in range(stages)]
     scratch += [vmem(shape(t), f32) for t in range(stages)]
     scratch += [dma((3, 3)) for t in range(2 * stages)]
-    smem = pl.BlockSpec(memory_space=pltpu.SMEM)
+    outside = pl.BlockSpec(memory_space=pltpu.HBM)
     anywhere = pl.BlockSpec(memory_space=pl.ANY)
     result = pl.pallas_call(
         functools.partial(kernel, dims),
         out_shape=jax.ShapeDtypeStruct((high, 5 * edge), f32),
-        in_specs=[smem, smem, smem, anywhere, anywhere],
-        out_specs=pl.BlockSpec(memory_space=pltpu.VMEM),
+        in_specs=[outside] * 5,
+        out_specs=anywhere,
         scratch_shapes=scratch,
         compiler_params=pltpu.CompilerParams(
-            collective_id=0, has_side_effects=True, vmem_limit_bytes=62 * 1024 * 1024),
-    )(a_cols.transpose(2, 0, 1), p_cols.transpose(0, 2, 1), coarse_slot.T, a_blocks.reshape(rows * links, block, block), p_blocks.reshape(rows * kp, block, block))
+            collective_id=0, has_side_effects=True, vmem_limit_bytes=44 * 1024 * 1024),
+    )(*(pltpu.with_memory_space_constraint(x, pltpu.HBM) for x in (
+        a_cols.transpose(2, 0, 1), p_cols.transpose(0, 2, 1), coarse_slot.T,
+        a_blocks.reshape(rows * links, block, block), p_blocks.reshape(rows * kp, block, block))))
     return result.reshape(1, owned, block, 5 * edge)
 
 

time: 57.3 us -> 54.1 us (0.944)
  Pallas kernels: 54.7 us -> 52.9 us
  local copies, waits for them, and re-layouts: 2.47 us -> 1.06 us
    pallas_call x1, Pallas kernels: 54.7 us -> 52.9 us  [on_device(): pl.pallas_call(functools.partial(kernel, dims), out_shape=jax.ShapeDtypeS...]
    unnamed x1, local copies, waits for them, and re-layouts: 2.47 us -> 1.06 us
where the time goes in v3:
time: 54.1 us; the launch traced here: 54 us
  Pallas kernels  52.9 us (98%)
  local copies, waits for them, and re-layouts  1.06 us (2%)
    pallas_call x1, Pallas kernels, on_device(): pl.pallas_call(functools.partial(kernel, dims), out_shape=jax.ShapeDtypeS...  52.9 us

profile of v3, /device:TPU:0, one launch (start us, length us, event | category | flops | bytes accessed | tf_op | source)
XLA Modules:
  0.0 54.0 jit_solution(16775328870929858474)
XLA Ops:
  0.0 52.9 %shard_map.55 = f32[128,2560]{1,0:T(8,128)S(1)} custom-call(s32[7,1,12]{2,1,0:T(1,128)} %bitcast.10, s32[4,4,96]{2,1,0:T(4,128)} %bitcast.9, s32[4,8]{1,0:T(4,128)} %bitcast.11, bf16[84,128,128]{2,1,0:T(8,128)(2,1)} %bitcast.7, bf16[48,128,128]{2,1,0:T(8,128)(2,1)} %bitcast.8), custom_call_target="tpu_custom_call" | custom-call | tf_op jit(solution)/shard_map/pallas_call | solution.py:327
  52.9 1.1 %copy.7 = f32[1,1,128,2560]{3,2,1,0:T(8,128)} copy(f32[1,1,128,2560]{3,2,1,0:T(8,128)S(1)} %bitcast.6) | data formatting | bytes 2621440
